TPU v7x, 32 devices: a whole 2x2x4 slice. The times are simulated.
32 devices in a mesh: dp: 2 (over x), tp2: 4 (over z), tp: 4 (over y, core).
Axes of the slice: x: 2, y: 2, z: 4, core: 2. Of those that a mesh axis runs over, the one named last changes fastest.
Arguments:
- hidden: bfloat16 [2048, 4096], P('dp'), parts along dimension 0
- w_gate: bfloat16 [4096, 14336], P(None, ('tp2', 'tp'))
- w_up: bfloat16 [4096, 14336], P(None, ('tp2', 'tp'))
- w_down: bfloat16 [14336, 4096], P(('tp2', 'tp'))
- norm_gain: float32 [4096], replicated
- w_vocab: bfloat16 [4096, 32768], P(None, ('tp2', 'tp'))
- temperature: float32 [2048], P('dp'), parts along dimension 0
- target_ids: int32 [2048], P('dp'), parts along dimension 0
Outputs:
- output 1: float32 [2048], P('dp'), parts along dimension 0
- output 2: float32 [2048], P('dp'), parts along dimension 0
- output 3: float32 [2048], P('dp'), parts along dimension 0
- output 4: bfloat16 [2048, 32768], P('dp', ('tp2', 'tp')), parts along dimension 0
There are 2 independent parts. A program takes and returns all parts, laid end to end along the dimension named above; an argument that names none is the same for every part.
All inputs are finite; a program needn't handle non-finite values.
Results may differ from a plain program's by a relative error of at most 0.00397131.
Values are sent between devices in bfloat16 or wider.
A program may use at most 1 GiB of HBM per device.

v0:
```python
import jax
import jax.numpy as jnp
from jax import lax
from jax.sharding import PartitionSpec as P

NORM_EPS = 1e-6


def solution(mesh):
    model_axes = ('tp2', 'tp')
    tp_size = mesh.shape['tp']

    def local_step(hidden, w_gate, w_up, w_down, norm_gain, w_vocab, value_a11, target_ids):
        gate_pre = jnp.dot(hidden, w_gate, preferred_element_type=jnp.float32)
        up_pre = jnp.dot(hidden, w_up, preferred_element_type=jnp.float32)
        hidden_act = (jax.nn.silu(gate_pre) * up_pre).astype(jnp.bfloat16)
        part_out = jnp.dot(hidden_act, w_down, preferred_element_type=jnp.float32).astype(jnp.bfloat16)
        mlp_out = lax.psum(part_out, model_axes)
        resid_sum = hidden.astype(jnp.float32) + mlp_out.astype(jnp.float32)
        inv_rms = lax.rsqrt(jnp.mean(resid_sum * resid_sum, axis=-1, keepdims=True) + NORM_EPS)
        normed = (norm_gain * resid_sum * inv_rms).astype(jnp.bfloat16)
        logits = jnp.dot(normed, w_vocab, preferred_element_type=jnp.float32) / value_a11[:, None]
        shard_cols = logits.shape[1]
        shard_index = lax.axis_index('tp2') * tp_size + lax.axis_index('tp')
        local_max = jnp.max(logits, axis=-1)
        shifted = jnp.exp(logits - local_max[:, None])
        local_sum = jnp.sum(shifted, axis=-1)
        local_moment = jnp.sum(shifted * logits, axis=-1)
        local_ids = target_ids - shard_index * shard_cols
        col_ids = jnp.arange(shard_cols, dtype=jnp.int32)
        local_target = jnp.sum(jnp.where(col_ids[None, :] == local_ids[:, None], logits, 0.0), axis=-1)
        global_max = lax.pmax(local_max, model_axes)
        rescale = jnp.exp(local_max - global_max)
        row_stats = jnp.stack([local_sum * rescale, local_moment * rescale, local_target], axis=0)
        totals = lax.psum(row_stats, model_axes)
        log_norm = global_max + jnp.log(totals[0])
        entropy = log_norm - totals[1] / totals[0]
        target_logp = totals[2] - log_norm
        logprobs = (logits - log_norm[:, None]).astype(jnp.bfloat16)
        return log_norm, entropy, target_logp, logprobs

    return jax.shard_map(
        local_step, mesh=mesh,
        in_specs=(P('dp', None), P(None, model_axes), P(None, model_axes), P(model_axes, None),
                  P(None), P(None, model_axes), P('dp'), P('dp')),
        out_specs=(P('dp'), P('dp'), P('dp'), P('dp', model_axes)),
        check_vma=False)
```

profile of v0, /device:TPU:0, one launch (start us, length us, event | category | flops | bytes accessed | tf_op | source)
XLA Modules:
  0.0 366.0 jit_solution(8359681730828034119)
XLA Ops:
  7.2 0.0 all-reduce.2.cloned.1.call-start
  7.2 14.6 %fusion.11 = f32[1024,896]{1,0:T(8,128)} fusion(bf16[1024,4096]{1,0:T(8,128)(2,1)} %param.8, bf16[4096,896]{1,0:T(8,128)(2,1)} %param.9), kind=kOutput, calls=%fused_computation.27 | convolution fusion | flops 7516192768 | bytes 19398656 | tf_op jit(solution)/shard_map/dot_general | solution.py:14
  21.8 26.7 %convolution_convert_fusion = bf16[1024,4096]{1,0:T(8,128)(2,1)} fusion(bf16[896,4096]{1,0:T(8,128)(2,1)} %param.11, f32[1024,896]{1,0:T(8,128)} %fusion.11, bf16[1024,4096]{1,0:T(8,128)(2,1)} %param.8, bf16[4096,896]{1,0:T(8,128)(2,1)} %param.10), kind=kOutput, calls=%fused_computation.12 | convolution fusion | flops 15042084864 | bytes 35127296 | tf_op jit(solution)/shard_map/dot_general | solution.py:17
  48.5 0.0 copy-start.1
  48.5 0.0 all-reduce.2.cloned.1.call-update
  48.5 0.7 copy-done.1
  49.2 0.0 copy-start.2
  49.2 0.0 copy-start.3
  49.2 172.0 %all-reduce.2.cloned.1.call-done = bf16[1024,4096]{1,0:T(8,128)(2,1)} async-done(((bf16[1024,4096]{1,0:T(8,128)(2,1)}), bf16[1024,4096]{1,0:T(8,128)(2,1)}) %all-reduce.2.cloned.1.call-update) | async-done | bytes 8388624 | tf_op jit(solution)/shard_map/psum | solution.py:18
  221.2 8.5 %multiply_reduce_fusion = f32[1024]{0:T(1024)S(1)} fusion(bf16[1024,4096]{1,0:T(8,128)(2,1)} %all-reduce.2.cloned.1.call-done, bf16[1024,4096]{1,0:T(8,128)(2,1)} %param.8), kind=kLoop, calls=%fused_computation.1 | loop fusion | flops 20970496 | bytes 16781312 | tf_op jit(solution)/shard_map/reduce_sum | solution.py:20
  229.7 0.0 copy-done.2
  229.7 0.0 copy-done.3
  229.7 27.4 %fusion.10 = (f32[1024]{0:T(1024)S(1)}, f32[1024,2048]{1,0:T(8,128)}) fusion(f32[1024]{0:T(1024)S(1)} %copy-done.3, bf16[4096,2048]{1,0:T(8,128)(2,1)} %param.13, bf16[1024,4096]{1,0:T(8,128)(2,1)} %all-reduce.2.cloned.1.call-done, bf16[1024,4096]{1,0:T(8,128)(2,1)} %param.8, f32[1024]{0:T(1024)S(1)} %add_rsqrt_fusion, f32[4096]{0:T(1024)S(1)} %copy-done.2), kind=kOutput, calls=%fused_computation.26 | convolution fusion | flops 17209229312 | bytes 41971712 | tf_op jit(solution)/shard_map/dot_general | solution.py:22
  257.1 31.9 %pmax.7 = f32[1024]{0:T(1024)S(1)} all-reduce(f32[1024]{0:T(1024)S(1)} %get-tuple-element.14), channel_id=1, replica_groups=mesh['dp'=2,'tp2'=4,'tp'=4] {'tp2','tp'}, use_global_device_ids=true, to_apply=%region_3.4 | all-reduce | flops 1024 | bytes 8192 | tf_op jit(solution)/shard_map/pmax | solution.py:32
  289.0 5.4 %fusion.1 = (f32[1024]{0:T(1024)S(1)}, f32[1024]{0:T(1024)S(1)}, f32[1024]{0:T(1024)S(1)}) fusion(f32[1024,2048]{1,0:T(8,128)} %get-tuple-element.15, f32[1024]{0:T(1024)S(1)} %get-tuple-element.14, s32[1024]{0:T(1024)S(1)} %broadcast_subtract_fusion), kind=kLoop, calls=%fused_computation.9 | loop fusion | flops 14676992 | bytes 8409088 | tf_op jit(solution)/shard_map/reduce_sum | solution.py:27
  294.5 57.6 %psum.15 = f32[3,1024]{1,0:T(4,128)S(1)} all-reduce(f32[3,1024]{1,0:T(4,128)S(1)} %pad_maximum_fusion), channel_id=1, replica_groups=mesh['dp'=2,'tp2'=4,'tp'=4] {'tp2','tp'}, use_global_device_ids=true, to_apply=%region_7.8 | all-reduce | flops 3072 | bytes 24576 | tf_op jit(solution)/shard_map/psum | solution.py:35
  352.1 0.6 fusion.9
  352.7 0.0 copy-start
  352.7 5.9 %subtract_convert_fusion = bf16[1024,2048]{1,0:T(8,128)(2,1)} fusion(f32[1024,2048]{1,0:T(8,128)} %get-tuple-element.15, f32[1024]{0:T(1024)S(1)} %get-tuple-element.8), kind=kLoop, calls=%fused_computation.4 | loop fusion | flops 4194304 | bytes 12587008 | tf_op jit(solution)/shard_map/convert_element_type | solution.py:39
  358.6 0.6 sub.36
  359.2 0.0 copy-done
  (5 shorter events, 0.1 us)
Async XLA Ops:
  7.2 214.0 %all-reduce.2.cloned.1.call-start = ((), (), s32[]{:S(2)}) async-start(), calls=%async_computation | async-start | bytes 16777216 | tf_op jit(solution)/shard_map/psum | solution.py:18
  48.5 0.7 copy-start.1
  49.2 180.5 %copy-start.2 = (f32[4096]{0:T(1024)S(1)}, f32[4096]{0:T(1024)}, u32[]{:S(2)}) copy-start(f32[4096]{0:T(1024)} %param.12) | copy-start | bytes 49156
  49.2 180.5 %copy-start.3 = (f32[1024]{0:T(1024)S(1)}, f32[1024]{0:T(1024)}, u32[]{:S(2)}) copy-start(f32[1024]{0:T(1024)} %param.14) | copy-start | bytes 12292
  352.7 6.5 %copy-start = (f32[1024]{0:T(1024)}, f32[1024]{0:T(1024)S(1)}, u32[]{:S(2)}) copy-start(f32[1024]{0:T(1024)S(1)} %get-tuple-element.8) | copy-start | bytes 12292
Sparse Core Ops, SparseCore 0:
  48.6 172.4 all-reduce.1
where the time goes:
time: 366 us
  waiting for transfers between devices  172 us (47%)
  blocking collectives  89.5 us (24%)
  matrix products  68.7 us (19%)
  other arithmetic  21.1 us (6%)
  between operations  14.1 us (4%)
    psum x1, waiting for transfers between devices, local_step(): mlp_out = lax.psum(part_out, model_axes)  172 us
    psum x1, blocking collectives, local_step(): totals = lax.psum(row_stats, model_axes)  57.6 us
    pmax x1, blocking collectives, local_step(): global_max = lax.pmax(local_max, model_axes)  31.9 us
    dot_general x1, matrix products, local_step(): jnp.dot(normed, w_vocab, preferred_element_type=jnp.float32)  27.4 us
    dot_general x1, matrix products, local_step(): jnp.dot(hidden_act, w_down, preferred_element_type=jnp.float32)  26.7 us
    dot_general x1, matrix products, local_step(): gate_pre = jnp.dot(hidden, w_gate, preferred_element_type=jnp.float32)  14.6 us
    reduce_sum x1, other arithmetic, local_step(): jnp.mean(resid_sum * resid_sum, axis=-1, keepdims=True) + NORM_EPS  8.53 us
  transfers between devices with their start and end apart: 1, of which 1 were waited for; matrix products, arithmetic and copies ran while one was open for 0% of the time, Pallas kernels for 0%

commit v1 on v0

v1 whole, which is shorter than its diff:
```python
import functools

import jax
import jax.numpy as jnp
from jax import lax
from jax.experimental import pallas as pl
from jax.experimental.pallas import tpu as pltpu
from jax.sharding import PartitionSpec as P

NORM_EPS = 1e-6
MESH = pl.DeviceIdType.MESH
F32 = jnp.float32
BF16 = jnp.bfloat16

CHUNK = 256
HALF = 128
PIECE = 16
UNITS = 6
GROUP = 16
OFF_A = (0, 2, 4, 6, 8, 10, 12, 13)
OFF_B = (0, 0, 2, 4, 6, 8, 10, 11)
VOCAB_AT = 23
FINAL_AT = 28


def kernel(num_chunks, hidden, w_gate, w_up, w_down, gain, w_vocab, temp, ids,
           logprobs, log_norm, entropy, target_logp,
           w1, w2, wv, hid, act, dsend, drecv, acc, zbuf, cbuf, ybuf, xbuf, hres, logits, stat, sbuf, outb,
           w_sem, w2_sem, wv_sem, hid_sem, hres_sem, out_sem, d_send, d_recv,
           y_send, y_recv, z_send, z_recv, c_recv, x_send, x_recv, xy_recv, xd_send, xd_recv, s_send, s_recv):
    dim = hidden.shape[1]
    ff = w_gate.shape[1]
    vocab = w_vocab.shape[1]
    vt = vocab // 4
    dt = dim // 8
    num_units = num_chunks * UNITS
    ft = ff // 128

    dp = lax.axis_index('dp')
    z = lax.axis_index('tp2')
    t = lax.axis_index('tp')
    y = t // 2
    c = t % 2
    me = z * 4 + t
    is_leaf = (z % 3) == 0
    is_center = (z % 3) != 0
    adj = 1 + z // 3
    leaf = 3 * (z // 2)
    other = 3 - z
    core_dev = (dp, z, y * 2 + 1 - c)
    y_dev = (dp, z, (1 - y) * 2 + c)
    adj_dev = (dp, adj, t)
    leaf_dev = (dp, leaf, t)
    other_dev = (dp, other, t)

    def w1_copies(n):
        col = pl.multiple_of(n * 128, 128)
        at = pl.multiple_of(n * 256, 256)
        return (pltpu.make_async_copy(w_gate.at[:, pl.ds(col, 128)], w1.at[:, pl.ds(at, 128)], w_sem.at[n, 0]),
                pltpu.make_async_copy(w_up.at[:, pl.ds(col, 128)], w1.at[:, pl.ds(at + 128, 128)], w_sem.at[n, 1]))

    def w2_copy():
        return pltpu.make_async_copy(w_down, w2, w2_sem)

    def wv_copy(n):
        q = n % 4
        b = n % 2
        return pltpu.make_async_copy(w_vocab.at[:, pl.ds(pl.multiple_of(q * vt, vt), vt)], wv.at[b], wv_sem.at[b])

    def hid_copies(i):
        own = pl.multiple_of(i * CHUNK + c * HALF, HALF)
        oth = pl.multiple_of(i * CHUNK + (1 - c) * HALF, HALF)
        return (pltpu.make_async_copy(hidden.at[pl.ds(own, HALF)], hid.at[pl.ds(0, HALF)], hid_sem.at[0]),
                pltpu.make_async_copy(hidden.at[pl.ds(oth, HALF)], hid.at[pl.ds(HALF, HALF)], hid_sem.at[1]))

    def out_copies(i):
        own = pl.multiple_of(i * CHUNK + c * HALF, HALF)
        oth = pl.multiple_of(i * CHUNK + (1 - c) * HALF, HALF)
        return (pltpu.make_async_copy(outb.at[pl.ds(0, HALF)], logprobs.at[pl.ds(own, HALF)], out_sem.at[0]),
                pltpu.make_async_copy(outb.at[pl.ds(HALF, HALF)], logprobs.at[pl.ds(oth, HALF)], out_sem.at[1]))

    def remote(src, dst, send, recv, dev):
        return pltpu.make_async_remote_copy(src_ref=src, dst_ref=dst, send_sem=send, recv_sem=recv,
                                            device_id=dev, device_id_type=MESH)

    def d_copy(i, part):
        cols = pl.ds(part * (dim // 2), dim // 2)
        return remote(dsend.at[:, cols], drecv.at[i, :, cols], d_send.at[part], d_recv.at[i, part], core_dev)

    def geo(u, kind):
        i = u // UNITS
        k = u % UNITS
        m = k % 3
        rs = 64 * (k // 3) + 16 * m + 16 * ((m + 1) // 2)
        if kind == 'A':
            return i, k, rs, rs + PIECE * y, 1 + k // 3
        return i, k, rs, rs, m

    def rows(start, n=PIECE):
        return pl.ds(pl.multiple_of(start, PIECE), n)

    def y_index(i, k, kind):
        return i * 4 + k // 3 + (0 if kind == 'A' else 2)

    def c_index(i, k, kind):
        return i * 3 + (0 if kind == 'A' else 1 + k // 3)

    def ya_copy(u):
        i, k, rs, mr, zo = geo(u, 'A')
        n = y_index(i, k, 'A')
        return remote(acc.at[i, rows(rs + PIECE * (1 - y))], ybuf.at[n], y_send.at[u], y_recv.at[n], y_dev)

    def yb_copy(u):
        i, k, rs, mr, zo = geo(u, 'B')
        n = y_index(i, k, 'B')
        return remote(acc.at[i, rows(mr)], ybuf.at[n], y_send.at[u], y_recv.at[n], y_dev)

    def z_copy(u, kind):
        i, k, rs, mr, zo = geo(u, kind)
        return remote(acc.at[i, rows(mr)], zbuf.at[u], z_send.at[u], z_recv.at[u], adj_dev)

    def c_copy(u, kind):
        i, k, rs, mr, zo = geo(u, kind)
        n = c_index(i, k, kind)
        return remote(acc.at[i, rows(mr)], cbuf.at[n], z_send.at[u], c_recv.at[n], other_dev)

    def x_copy(u, kind, which):
        i, k, rs, mr, zo = geo(u, kind)
        block = xbuf.at[i, rows(mr)]
        dev = (leaf_dev, other_dev, y_dev)[which]
        recv = xy_recv.at[u // 3] if which == 2 else x_recv.at[u]
        return remote(block, block, x_send.at[u, which], recv, dev)

    def xy_wait(u):
        i, k, rs, mr, zo = geo(u, 'A')
        block = xbuf.at[i, rows(rs + PIECE * (1 - y))]
        return remote(block, block, x_send.at[u, 2], xy_recv.at[u // 3], y_dev)

    def xd_copy(u, kind):
        i, k, rs, mr, zo = geo(u, kind)
        n = 2 * PIECE if kind == 'A' else PIECE
        return remote(xbuf.at[i, rows(rs, n)], xbuf.at[i, rows(HALF + rs, n)], xd_send.at[u], xd_recv.at[u], core_dev)

    def hres_copy(u, kind):
        i, k, rs, mr, zo = geo(u, kind)
        row = pl.multiple_of(i * CHUNK + c * HALF + mr, PIECE)
        return pltpu.make_async_copy(hidden.at[pl.ds(row, PIECE)], hres.at[u % 8], hres_sem.at[u % 8])

    cb = min(dim, 1024)

    def add_rows(i, start, n, *terms):
        for j in range(dim // cb):
            cols = pl.ds(j * cb, cb)
            total = acc[i, rows(start, n), cols].astype(F32)
            for ref in terms:
                total = total + ref[:, cols].astype(F32)
            acc[i, rows(start, n), cols] = total.astype(BF16)

    def norm_rows(u, kind, *terms):
        i, k, rs, mr, zo = geo(u, kind)
        slot = hres.at[u % 8]
        hres_copy(u, kind).wait()
        square = jnp.zeros((PIECE, 128), F32)
        for j in range(dim // cb):
            cols = pl.ds(j * cb, cb)
            total = acc[i, rows(mr), cols].astype(F32)
            for ref in terms:
                total = total + ref[:, cols].astype(F32)
            resid = slot[:, cols].astype(F32) + total.astype(BF16).astype(F32)
            sq = resid * resid
            for b in range(cb // 128):
                square = square + sq[:, b * 128:(b + 1) * 128]
            xbuf[i, rows(mr), cols] = total.astype(BF16)
        inv = lax.rsqrt(jnp.sum(square, axis=-1, keepdims=True) / dim + NORM_EPS)
        for j in range(dim // cb):
            cols = pl.ds(j * cb, cb)
            resid = slot[:, cols].astype(F32) + xbuf[i, rows(mr), cols].astype(F32)
            xbuf[i, rows(mr), cols] = (gain[:, cols] * resid * inv).astype(BF16)

    def s_copy(i, d):
        peer = (me + d) % GROUP
        return remote(sbuf.at[i, 0], sbuf.at[i, d], s_send.at[i], s_recv.at[i], (dp, peer // 4, peer % 4))

    def s_wait(i):
        block = sbuf.at[i, pl.ds(1, GROUP - 1)]
        return remote(block, block, s_send.at[i], s_recv.at[i], core_dev)

    for cp in hid_copies(0):
        cp.start()

    def load_w1(n, _):
        for cp in w1_copies(n):
            cp.start()
        return 0
    lax.fori_loop(0, ft, load_w1, 0)
    w2_copy().start()
    wv_copy(0).start()
    wv_copy(1).start()

    barrier = pltpu.get_barrier_semaphore()

    def greet(d, _):
        peer = (me + d) % GROUP
        pl.semaphore_signal(barrier, inc=1, device_id=(dp, peer // 4, peer % 4), device_id_type=MESH)
        return 0
    lax.fori_loop(1, GROUP, greet, 0)
    pl.semaphore_wait(barrier, GROUP - 1)

    def gate_up(i, j):
        def tile(n, _):
            @pl.when(i == 0)
            def _():
                for cp in w1_copies(n):
                    cp.wait()
            at = pl.multiple_of(n * 256, 256)
            both = jnp.dot(hid[...], w1[:, pl.ds(at, 256)], preferred_element_type=F32)
            g = both[:, :128]
            act[:, pl.ds(pl.multiple_of(n * 128, 128), 128)] = (jax.nn.silu(g) * both[:, 128:]).astype(BF16)
            return 0
        per = -(-ft // 4)
        lax.fori_loop(j * per, jnp.minimum(j * per + per, ft), tile, 0)

    def down(i, part):
        def tile(n, _):
            cols = pl.ds(pl.multiple_of(n * dt, dt), dt)
            out = jnp.dot(act[...], w2[:, cols], preferred_element_type=F32).astype(BF16)
            acc[i, :, cols] = out[:HALF]
            dsend[:, cols] = out[HALF:]
            return 0
        lax.fori_loop(part * 4, part * 4 + 4, tile, 0)

    def mlp(s):
        i = s // UNITS
        j = s % UNITS

        @pl.when(j == 0)
        def _():
            for cp in hid_copies(i):
                cp.wait()

        @pl.when(j < 4)
        def _():
            gate_up(i, j)

        @pl.when((j == 3) & (i + 1 < num_chunks))
        def _():
            for cp in hid_copies(i + 1):
                cp.start()

        @pl.when((j == 4) & (i == 0))
        def _():
            w2_copy().wait()

        @pl.when((j == 4) & (i > 0))
        def _():
            d_copy(i - 1, 0).wait_send()
            d_copy(i - 1, 1).wait_send()

        @pl.when(j >= 4)
        def _():
            down(i, j - 4)

        @pl.when(j == 4)
        def _():
            d_copy(i, 0).start()

        @pl.when(j == 5)
        def _():
            d_copy(i, 1).start()

    def column(row_ref, i, h):
        r = row_ref[pl.ds(2 * i + (c if h == 0 else 1 - c), 1), :].astype(F32)
        return jnp.transpose(jnp.broadcast_to(r, (128, 128)))

    lanes = 128
    rb = 32

    def vocab_step(i, q):
        n = i * 4 + q
        wv_copy(n).wait()
        col = pl.multiple_of(q * vt, vt)
        logits[:, pl.ds(col, vt)] = jnp.dot(xbuf[i], wv[n % 2], preferred_element_type=F32)

        @pl.when(n + 2 < num_chunks * 4)
        def _():
            wv_copy(n + 2).start()

        @pl.when(q == 0)
        def _():
            for h in range(2):
                r = pl.ds(h * HALF, HALF)
                stat[0, r] = jnp.full((HALF, lanes), -jnp.inf, F32)
                stat[1, r] = jnp.zeros((HALF, lanes), F32)
                stat[2, r] = jnp.zeros((HALF, lanes), F32)
                stat[3, r] = jnp.zeros((HALF, lanes), F32)
                stat[4, r] = 1.0 / column(temp, i, h)
                stat[5, r] = column(ids, i, h) - (me * vocab).astype(F32)

        def block(b, _):
            r = pl.ds(pl.multiple_of(b * rb, rb), rb)
            inv_t = stat[4, r]
            want = stat[5, r] - lax.broadcasted_iota(jnp.int32, (rb, lanes), 1).astype(F32) - (q * vt).astype(F32)
            old = stat[0, r]
            top = old
            parts = []
            target = stat[3, r]
            for g in range(vt // lanes):
                cols = pl.ds(pl.multiple_of(col + g * lanes, lanes), lanes)
                lg = logits[r, cols] * inv_t
                logits[r, cols] = lg
                top = jnp.maximum(top, lg)
                target = target + jnp.where(want == float(g * lanes), lg, 0.0)
                parts.append(lg)
            scale = jnp.exp(old - top)
            total = stat[1, r] * scale
            moment = stat[2, r] * scale
            for lg in parts:
                e = jnp.exp(lg - top)
                total = total + e
                moment = moment + e * lg
            stat[0, r] = top
            stat[1, r] = total
            stat[2, r] = moment
            stat[3, r] = target
            return 0
        lax.fori_loop(0, CHUNK // rb, block, 0)

        @pl.when(q == 3)
        def _():
            for h in range(2):
                r = pl.ds(h * HALF, HALF)
                top = stat[0, r]
                best = jnp.max(top, axis=-1, keepdims=True)
                w = jnp.exp(top - best)
                total = jnp.sum(stat[1, r] * w, axis=-1, keepdims=True)
                moment = jnp.sum(stat[2, r] * w, axis=-1, keepdims=True)
                target = jnp.sum(stat[3, r], axis=-1, keepdims=True)
                lane = lax.broadcasted_iota(jnp.int32, (HALF, lanes), 1)
                packed = jnp.where(lane == 0, best, jnp.where(lane == 1, total, jnp.where(lane == 2, moment, target)))
                turned = jnp.transpose(packed)[:8]
                at = pl.multiple_of((c if h == 0 else 1 - c) * HALF, HALF)
                sbuf[i, 0, :, pl.ds(at, HALF)] = turned
            for d in range(1, GROUP):
                s_copy(i, d).start()

    def final_step(i):
        s_wait(i).wait_recv()
        top = sbuf[i, 0, 0:1, :]
        for d in range(1, GROUP):
            top = jnp.maximum(top, sbuf[i, d, 0:1, :])
        total = jnp.zeros((1, CHUNK), F32)
        moment = jnp.zeros((1, CHUNK), F32)
        target = jnp.zeros((1, CHUNK), F32)
        for d in range(GROUP):
            w = jnp.exp(sbuf[i, d, 0:1, :] - top)
            total = total + w * sbuf[i, d, 1:2, :]
            moment = moment + w * sbuf[i, d, 2:3, :]
            target = target + sbuf[i, d, 3:4, :]
        norm = top + jnp.log(total)
        ent = norm - moment / total
        tlp = target - norm
        for h in range(2):
            r = pl.ds(2 * i + h, 1)
            cols = slice(h * HALF, (h + 1) * HALF)
            log_norm[r, :] = norm[:, cols]
            entropy[r, :] = ent[:, cols]
            target_logp[r, :] = tlp[:, cols]

        @pl.when(i > 0)
        def _():
            for cp in out_copies(i - 1):
                cp.wait()
        for h in range(2):
            row = column(log_norm, i, h)
            stat[0, pl.ds(h * HALF, HALF)] = row

        def block(b, _):
            r = pl.ds(pl.multiple_of(b * rb, rb), rb)
            ln = stat[0, r]
            for g in range(vocab // lanes):
                cols = pl.ds(g * lanes, lanes)
                outb[r, cols] = (logits[r, cols] - ln).astype(BF16)
            return 0
        lax.fori_loop(0, CHUNK // rb, block, 0)
        for cp in out_copies(i):
            cp.start()

    def unit(s, h, kind, body):
        off = (OFF_A if kind == 'A' else OFF_B)[h]
        u = s - UNITS - off
        fit = (u % 3) == 0 if kind == 'A' else (u % 3) != 0

        @pl.when((u >= 0) & (u < num_units) & fit)
        def _():
            body(u)

    def first(kind):
        def body(u):
            i, k, rs, mr, zo = geo(u, kind)
            if kind == 'A':
                @pl.when(k == 0)
                def _():
                    d_copy(i, 0).wait_recv()
                    d_copy(i, 1).wait_recv()
                add_rows(i, rs, 2 * PIECE, drecv.at[i, rows(rs, 2 * PIECE)])
                ya_copy(u).start()
            else:
                add_rows(i, rs, PIECE, drecv.at[i, rows(rs)])

                @pl.when(is_leaf)
                def _():
                    z_copy(u, kind).start()
        return body

    def after_y(u):
        i, k, rs, mr, zo = geo(u, 'A')
        ya_copy(u).wait_recv()
        add_rows(i, mr, PIECE, ybuf.at[y_index(i, k, 'A')])

        @pl.when(is_leaf)
        def _():
            z_copy(u, 'A').start()

    def after_z(kind):
        def body(u):
            i, k, rs, mr, zo = geo(u, kind)

            @pl.when(z == 3 - zo)
            def _():
                z_copy(u, kind).wait_recv()
                add_rows(i, mr, PIECE, zbuf.at[u])
                c_copy(u, kind).start()

            @pl.when(z == zo)
            def _():
                hres_copy(u, kind).start()
        return body

    def spread(u, kind):
        x_copy(u, kind, 0).start()
        x_copy(u, kind, 1).start()
        if kind == 'A':
            x_copy(u, kind, 2).start()

    def after_c(kind):
        def body(u):
            i, k, rs, mr, zo = geo(u, kind)

            @pl.when(z == zo)
            def _():
                z_copy(u, kind).wait_recv()
                c_copy(u, kind).wait_recv()
                n = c_index(i, k, kind)
                if kind == 'A':
                    norm_rows(u, kind, zbuf.at[u], cbuf.at[n])
                    spread(u, kind)
                else:
                    add_rows(i, mr, PIECE, zbuf.at[u], cbuf.at[n])
                    yb_copy(u).start()
        return body

    def after_yb(u):
        i, k, rs, mr, zo = geo(u, 'B')

        @pl.when(z == zo)
        def _():
            yb_copy(u).wait_recv()
            norm_rows(u, 'B', ybuf.at[y_index(i, k, 'B')])
            spread(u, 'B')

    def near(kind):
        def body(u):
            i, k, rs, mr, zo = geo(u, kind)

            @pl.when(z == 3 - zo)
            def _():
                x_copy(u, kind, 0).wait_recv()
                x_copy(u, kind, 0).start()
                if kind == 'A':
                    x_copy(u, kind, 2).start()

            @pl.when(z == 3 * (zo - 1))
            def _():
                x_copy(u, kind, 0).wait_recv()
                if kind == 'A':
                    x_copy(u, kind, 2).start()
        return body

    def far(kind):
        def body(u):
            i, k, rs, mr, zo = geo(u, kind)

            @pl.when(z == 3 * (2 - zo))
            def _():
                x_copy(u, kind, 0).wait_recv()
                if kind == 'A':
                    x_copy(u, kind, 2).start()
            if kind == 'B':
                xd_copy(u, kind).start()
        return body

    def after_xy(u):
        xy_wait(u).wait_recv()
        xd_copy(u, 'A').start()

    def after_xd(kind):
        def body(u):
            xd_copy(u, kind).wait_recv()
        return body

    def slot(s, _):
        unit(s, 7, 'A', after_xd('A'))
        unit(s, 7, 'B', after_xd('B'))
        unit(s, 6, 'A', after_xy)
        unit(s, 6, 'B', far('B'))
        unit(s, 5, 'A', far('A'))
        unit(s, 5, 'B', near('B'))
        unit(s, 4, 'A', near('A'))
        unit(s, 4, 'B', after_yb)
        unit(s, 3, 'A', after_c('A'))
        unit(s, 3, 'B', after_c('B'))
        unit(s, 2, 'A', after_z('A'))
        unit(s, 2, 'B', after_z('B'))
        unit(s, 1, 'A', after_y)
        unit(s, 0, 'A', first('A'))
        unit(s, 0, 'B', first('B'))

        f = s - FINAL_AT

        @pl.when((f >= 0) & (f % UNITS == 0))
        def _():
            final_step(f // UNITS)

        v = s - VOCAB_AT

        @pl.when((v >= 0) & (v % UNITS < 4) & (v < UNITS * num_chunks))
        def _():
            vocab_step(v // UNITS, v % UNITS)

        @pl.when(s < UNITS * num_chunks)
        def _():
            mlp(s)
        return 0

    last = UNITS * (num_chunks - 1) + FINAL_AT
    lax.fori_loop(0, last + 1, slot, 0)

    for cp in out_copies(num_chunks - 1):
        cp.wait()
    d_copy(num_chunks - 1, 0).wait_send()
    d_copy(num_chunks - 1, 1).wait_send()

    def drain_unit(u, kind):
        i, k, rs, mr, zo = geo(u, kind)
        xd_copy(u, kind).wait_send()
        if kind == 'A':
            ya_copy(u).wait_send()
            x_copy(u, kind, 2).wait_send()

        @pl.when(is_leaf)
        def _():
            z_copy(u, kind).wait_send()

        @pl.when(z == 3 - zo)
        def _():
            c_copy(u, kind).wait_send()
            x_copy(u, kind, 0).wait_send()

        @pl.when(z == zo)
        def _():
            if kind == 'B':
                yb_copy(u).wait_send()
            x_copy(u, kind, 0).wait_send()
            x_copy(u, kind, 1).wait_send()

    def drain(n, _):
        drain_unit(3 * n, 'A')
        drain_unit(3 * n + 1, 'B')
        drain_unit(3 * n + 2, 'B')
        return 0
    lax.fori_loop(0, num_units // 3, drain, 0)

    def drain_stats(i, _):
        s_wait(i).wait_send()
        return 0
    lax.fori_loop(0, num_chunks, drain_stats, 0)


def fused(hidden, w_gate, w_up, w_down, gain, w_vocab, temp, ids):
    rows, dim = hidden.shape
    ff = w_gate.shape[1]
    vocab = w_vocab.shape[1]
    nc = rows // CHUNK
    nu = nc * UNITS
    vm = pl.BlockSpec(memory_space=pltpu.VMEM)
    hbm = pl.BlockSpec(memory_space=pl.ANY)
    dma = pltpu.SemaphoreType.DMA
    small = jax.ShapeDtypeStruct((rows // 128, 128), F32)
    return pl.pallas_call(
        functools.partial(kernel, nc),
        out_shape=(jax.ShapeDtypeStruct((rows, vocab), BF16), small, small, small),
        in_specs=[hbm, hbm, hbm, hbm, vm, hbm, vm, vm],
        out_specs=(hbm, vm, vm, vm),
        scratch_shapes=[
            pltpu.VMEM((dim, 2 * ff), BF16),
            pltpu.VMEM((ff, dim), BF16),
            pltpu.VMEM((2, dim, vocab // 4), BF16),
            pltpu.VMEM((CHUNK, dim), BF16),
            pltpu.VMEM((CHUNK, ff), BF16),
            pltpu.VMEM((HALF, dim), BF16),
            pltpu.VMEM((nc, HALF, dim), BF16),
            pltpu.VMEM((nc, HALF, dim), BF16),
            pltpu.VMEM((nu, PIECE, dim), BF16),
            pltpu.VMEM((nc * 3, PIECE, dim), BF16),
            pltpu.VMEM((nc * 4, PIECE, dim), BF16),
            pltpu.VMEM((nc, CHUNK, dim), BF16),
            pltpu.VMEM((8, PIECE, dim), BF16),
            pltpu.VMEM((CHUNK, vocab), F32),
            pltpu.VMEM((6, CHUNK, 128), F32),
            pltpu.VMEM((nc, GROUP, 8, CHUNK), F32),
            pltpu.VMEM((CHUNK, vocab), BF16),
            dma((ff // 128, 2)), dma, dma((2,)), dma((2,)), dma((8,)), dma((2,)), dma((2,)), dma((nc, 2)),
            dma((nu,)), dma((nc * 4,)), dma((nu,)), dma((nu,)), dma((nc * 3,)), dma((nu, 3)), dma((nu,)),
            dma((nu // 3,)), dma((nu,)), dma((nu,)), dma((nc,)), dma((nc,)),
        ],
        compiler_params=pltpu.CompilerParams(collective_id=0, has_side_effects=True, vmem_limit_bytes=67043328),
        cost_estimate=pl.CostEstimate(flops=2 * rows * dim * (3 * ff + vocab),
                                      bytes_accessed=2 * dim * (3 * ff + 4 * vocab + rows),
                                      transcendentals=rows * vocab),
        name='step_tail',
    )(hidden, w_gate, w_up, w_down, gain, w_vocab, temp, ids)


def solution(mesh):
    model_axes = ('tp2', 'tp')

    def local_step(hidden, w_gate, w_up, w_down, norm_gain, w_vocab, temperature, target_ids):
        rows = hidden.shape[0]
        logprobs, log_norm, entropy, target_logp = fused(
            hidden, w_gate, w_up, w_down, norm_gain[None, :], w_vocab,
            temperature.reshape(rows // 128, 128), target_ids.reshape(rows // 128, 128))
        return log_norm.reshape(rows), entropy.reshape(rows), target_logp.reshape(rows), logprobs

    return jax.shard_map(
        local_step, mesh=mesh,
        in_specs=(P('dp', None), P(None, model_axes), P(None, model_axes), P(model_axes, None),
                  P(None), P(None, model_axes), P('dp'), P('dp')),
        out_specs=(P('dp'), P('dp'), P('dp'), P('dp', model_axes)),
        check_vma=False)
```

time: 366 us -> 167 us (0.46)
  waiting for transfers between devices: 172 us -> 0 us
  Pallas kernels: 0 us -> 158 us
  blocking collectives: 89.5 us -> 0 us
  matrix products: 68.7 us -> 0 us
  other arithmetic: 21.1 us -> 0 us
  between operations: 14.1 us -> 0.64 us
  local copies, waits for them, and re-layouts: 0.67 us -> 8.59 us
    psum x1 -> x0, waiting for transfers between devices: 172 us -> none  [local_step(): mlp_out = lax.psum(part_out, model_axes)]
    pallas_call x0 -> x1, Pallas kernels: none -> 158 us  [fused(): pl.pallas_call(functools.partial(kernel, nc), out_shape=(jax.ShapeDtypeSt...]
    dot_general x3 -> x0, matrix products: 68.7 us -> none  [the longest x1 27.4 us: local_step(): jnp.dot(normed, w_vocab, preferred_element_type=jnp.float32)]
    psum x1 -> x0, blocking collectives: 57.6 us -> none  [local_step(): totals = lax.psum(row_stats, model_axes)]
    pmax x1 -> x0, blocking collectives: 31.9 us -> none  [local_step(): global_max = lax.pmax(local_max, model_axes)]
    reduce_sum x2 -> x0, other arithmetic: 13.9 us -> none  [the longest x1 8.53 us: local_step(): jnp.mean(resid_sum * resid_sum, axis=-1, keepdims=True) + NORM_EPS]
    unnamed x8 -> x4, local copies, waits for them, and re-layouts: 0.67 us -> 8.59 us
    convert_element_type x1 -> x0, other arithmetic: 5.9 us -> none  [local_step(): logprobs = (logits - log_norm[:, None]).astype(jnp.bfloat16)]
  transfers between devices with their start and end apart: 1 -> 0, of which waited for: 1 -> 0; matrix products, arithmetic and copies ran while one was open for 0% -> 0% of each run, Pallas kernels for 0% -> 0%
where the time goes in v1:
time: 167 us
  Pallas kernels  158 us (95%)
  local copies, waits for them, and re-layouts  8.59 us (5%)
    pallas_call x1, Pallas kernels, fused(): pl.pallas_call(functools.partial(kernel, nc), out_shape=(jax.ShapeDtypeSt...  158 us
    unnamed x4, local copies, waits for them, and re-layouts  8.59 us

profile of v1, /device:TPU:0, one launch (start us, length us, event | category | flops | bytes accessed | tf_op | source)
XLA Modules:
  0.0 166.8 jit_solution(12481681716206937926)
XLA Ops:
  0.6 157.6 %step_tail.1 = (bf16[1024,2048]{1,0:T(8,128)(2,1)}, f32[8,128]{1,0:T(8,128)}, f32[8,128]{1,0:T(8,128)}, f32[8,128]{1,0:T(8,128)}) custom-call(bf16[1024,4096]{1,0:T(8,128)(2,1)} %hidden.1, bf16[4096,896]{1,0:T(8,128)(2,1)} %w_gate.1, bf16[4096,896]{1,0:T(8,128)(2,1)} %w_up.1, bf16[896,4096]{1,0:T(8,128)(2,1)} %w_down.1, f32[1,4096]{1,0:T(1,128)} %bitcast.9, ...), custom_call_target="tpu_custom_call" | custom-call | flops 39728447488 | bytes 97517568 | tf_op jit(solution)/shard_map/step_tail/pallas_call | solution.py:599
  158.3 1.3 copy.16
  159.5 1.3 copy.17
  160.8 1.3 copy.18
  162.1 4.8 %copy.19 = bf16[1024,2048]{1,0:T(8,128)(2,1)} copy(bf16[1024,2048]{1,0:T(8,128)(2,1)} %get-tuple-element.19) | data formatting | bytes 8388608

commit v2 on v1

v2 whole, which is shorter than its diff:
```python
import functools

import jax
import jax.numpy as jnp
from jax import lax
from jax.experimental import pallas as pl
from jax.experimental.pallas import tpu as pltpu
from jax.sharding import PartitionSpec as P

NORM_EPS = 1e-6
MESH = pl.DeviceIdType.MESH
F32 = jnp.float32
BF16 = jnp.bfloat16

CHUNK = 256
HALF = 128
PIECE = 16
UNITS = 6
GROUP = 16
KINDS = 'ABBABB'
POS_UNIT = (
    (6.295, 9.934, 14.066, 22.525, 29.115, 34.033, 39.443, 42.984, 46.131),
    (6.59, 9.639, 19.18, 22.721, 26.951, 35.213, 43.672, 44.754),
    (7.377, 10.23, 14.164, 17.508, 21.148, 25.77, 33.738, 45.049),
    (7.475, 11.607, 17.902, 23.705, 29.803, 36.885, 39.541, 42.492, 47.016),
    (8.262, 12.393, 18.098, 22.623, 27.246, 33.344, 37.869, 46.426),
    (8.852, 13.574, 19.279, 23.311, 30.689, 38.557, 42.787, 46.918),
)
POS_MLP = (0.197, 1.967, 2.361, 2.656, 4.328, 4.82)
POS_VOCAB = (48, 49.082, 50.459, 53.41)
POS_FINAL = 57.836

def kernel(num_chunks, hidden, w_gate, w_up, w_down, gain, w_vocab, temp, ids,
           logprobs, log_norm, entropy, target_logp,
           w1, w2, wv, hid, act, dsend, drecv, acc, zbuf, cbuf, ybuf, xbuf, hres, logits, stat, sbuf, outb,
           w_sem, w2_sem, wv_sem, hid_sem, hres_sem, out_sem, d_send, d_recv,
           y_send, y_recv, z_send, z_recv, c_recv, x_send, x_recv, xy_recv, xd_send, xd_recv, s_send, s_recv):
    dim = hidden.shape[1]
    ff = w_gate.shape[1]
    vocab = w_vocab.shape[1]
    vt = vocab // 4
    dt = dim // 8
    num_units = num_chunks * UNITS
    ft = ff // 128

    dp = lax.axis_index('dp')
    z = lax.axis_index('tp2')
    t = lax.axis_index('tp')
    y = t // 2
    c = t % 2
    me = z * 4 + t
    core_dev = (dp, z, y * 2 + 1 - c)
    y_dev = (dp, z, (1 - y) * 2 + c)
    def dist(zo):
        return z if zo < 2 else 3 - z

    def step_dev(zo, way):
        there = z - way if zo < 2 else z + way
        return (dp, jnp.clip(there, 0, 3), t)

    def w1_copies(n):
        col = pl.multiple_of(n * 128, 128)
        at = pl.multiple_of(n * 256, 256)
        return (pltpu.make_async_copy(w_gate.at[:, pl.ds(col, 128)], w1.at[:, pl.ds(at, 128)], w_sem.at[n, 0]),
                pltpu.make_async_copy(w_up.at[:, pl.ds(col, 128)], w1.at[:, pl.ds(at + 128, 128)], w_sem.at[n, 1]))

    def w2_copy():
        return pltpu.make_async_copy(w_down, w2, w2_sem)

    def wv_copy(n):
        q = n % 4
        b = n % 2
        return pltpu.make_async_copy(w_vocab.at[:, pl.ds(pl.multiple_of(q * vt, vt), vt)], wv.at[b], wv_sem.at[b])

    def hid_copies(i):
        own = pl.multiple_of(i * CHUNK + c * HALF, HALF)
        oth = pl.multiple_of(i * CHUNK + (1 - c) * HALF, HALF)
        return (pltpu.make_async_copy(hidden.at[pl.ds(own, HALF)], hid.at[pl.ds(0, HALF)], hid_sem.at[0]),
                pltpu.make_async_copy(hidden.at[pl.ds(oth, HALF)], hid.at[pl.ds(HALF, HALF)], hid_sem.at[1]))

    def out_copies(i):
        own = pl.multiple_of(i * CHUNK + c * HALF, HALF)
        oth = pl.multiple_of(i * CHUNK + (1 - c) * HALF, HALF)
        return (pltpu.make_async_copy(outb.at[pl.ds(0, HALF)], logprobs.at[pl.ds(own, HALF)], out_sem.at[0]),
                pltpu.make_async_copy(outb.at[pl.ds(HALF, HALF)], logprobs.at[pl.ds(oth, HALF)], out_sem.at[1]))

    def remote(src, dst, send, recv, dev):
        return pltpu.make_async_remote_copy(src_ref=src, dst_ref=dst, send_sem=send, recv_sem=recv,
                                            device_id=dev, device_id_type=MESH)

    def d_copy(i, part):
        start = part * (dim // 2)
        cols = pl.ds(start if isinstance(part, int) else pl.multiple_of(start, dim // 2), dim // 2)
        return remote(dsend.at[:, cols], drecv.at[i, :, cols], d_send.at[part], d_recv.at[i, part], core_dev)

    def geo(u, kind):
        i, k = u
        m = k % 3
        rs = 64 * (k // 3) + 16 * m + 16 * ((m + 1) // 2)
        if kind == 'A':
            return i, k, rs, rs + PIECE * y, 3 * (k // 3)
        return i, k, rs, rs, m if kind == 'C' else 3 * (m - 1)

    def flat(u):
        return u[0] * UNITS + u[1]

    def rows(start, n=PIECE):
        return pl.ds(pl.multiple_of(start, PIECE), n)

    def y_index(i, k, kind):
        return i * 4 + k // 3 + (0 if kind == 'A' else 2)

    def ya_copy(u):
        i, k, rs, mr, zo = geo(u, 'A')
        n = y_index(i, k, 'A')
        return remote(acc.at[i, rows(rs + PIECE * (1 - y))], ybuf.at[n], y_send.at[flat(u)], y_recv.at[n], y_dev)

    def yb_copy(u, kind):
        i, k, rs, mr, zo = geo(u, kind)
        n = y_index(i, k, 'B')
        return remote(acc.at[i, rows(mr)], ybuf.at[n], y_send.at[flat(u)], y_recv.at[n], y_dev)

    def z_copy(u, kind):
        i, k, rs, mr, zo = geo(u, kind)
        return remote(acc.at[i, rows(mr)], zbuf.at[flat(u)], z_send.at[flat(u)], z_recv.at[flat(u)], step_dev(zo, 1))

    def x_copy(u, kind):
        i, k, rs, mr, zo = geo(u, kind)
        block = xbuf.at[i, rows(mr)]
        return remote(block, block, x_send.at[flat(u), 0], x_recv.at[flat(u)], step_dev(zo, -1))

    def c_copy(u):
        i, k, rs, mr, zo = geo(u, 'C')
        return remote(acc.at[i, rows(mr)], cbuf.at[i], z_send.at[flat(u)], c_recv.at[i], step_dev(zo, -1))

    def xn_copy(u):
        i, k, rs, mr, zo = geo(u, 'C')
        block = xbuf.at[i, rows(mr)]
        return remote(block, block, x_send.at[flat(u), 1], x_recv.at[flat(u)], step_dev(zo, 1))

    def xy_copy(u):
        i, k, rs, mr, zo = geo(u, 'A')
        block = xbuf.at[i, rows(mr)]
        return remote(block, block, x_send.at[flat(u), 1], xy_recv.at[flat(u) // 3], y_dev)

    def xy_wait(u):
        i, k, rs, mr, zo = geo(u, 'A')
        block = xbuf.at[i, rows(rs + PIECE * (1 - y))]
        return remote(block, block, x_send.at[flat(u), 1], xy_recv.at[flat(u) // 3], y_dev)

    def xd_copy(u, kind):
        i, k, rs, mr, zo = geo(u, kind)
        n = 2 * PIECE if kind == 'A' else PIECE
        return remote(xbuf.at[i, rows(rs, n)], xbuf.at[i, rows(HALF + rs, n)], xd_send.at[flat(u)], xd_recv.at[flat(u)], core_dev)

    def hres_copy(u, kind):
        i, k, rs, mr, zo = geo(u, kind)
        row = pl.multiple_of(i * CHUNK + c * HALF + mr, PIECE)
        return pltpu.make_async_copy(hidden.at[pl.ds(row, PIECE)], hres.at[flat(u) % 12], hres_sem.at[flat(u) % 12])

    cb = min(dim, 1024)

    def add_rows(i, start, n, *terms):
        for j in range(dim // cb):
            cols = pl.ds(j * cb, cb)
            total = acc[i, rows(start, n), cols].astype(F32)
            for ref in terms:
                total = total + ref[:, cols].astype(F32)
            acc[i, rows(start, n), cols] = total.astype(BF16)

    def norm_rows(u, kind, *terms):
        i, k, rs, mr, zo = geo(u, kind)
        slot = hres.at[flat(u) % 12]
        hres_copy(u, kind).wait()
        square = jnp.zeros((PIECE, 128), F32)
        for j in range(dim // cb):
            cols = pl.ds(j * cb, cb)
            total = acc[i, rows(mr), cols].astype(F32)
            for ref in terms:
                total = total + ref[:, cols].astype(F32)
            resid = slot[:, cols].astype(F32) + total.astype(BF16).astype(F32)
            sq = resid * resid
            for b in range(cb // 128):
                square = square + sq[:, b * 128:(b + 1) * 128]
            xbuf[i, rows(mr), cols] = total.astype(BF16)
        inv = lax.rsqrt(jnp.sum(square, axis=-1, keepdims=True) / dim + NORM_EPS)
        for j in range(dim // cb):
            cols = pl.ds(j * cb, cb)
            resid = slot[:, cols].astype(F32) + xbuf[i, rows(mr), cols].astype(F32)
            xbuf[i, rows(mr), cols] = (gain[:, cols] * resid * inv).astype(BF16)

    def s_copy(i, d):
        peer = (me + d) % GROUP
        return remote(sbuf.at[i, 0], sbuf.at[i, d], s_send.at[i], s_recv.at[i], (dp, peer // 4, peer % 4))

    def s_wait(i):
        block = sbuf.at[i, pl.ds(1, GROUP - 1)]
        return remote(block, block, s_send.at[i], s_recv.at[i], core_dev)

    for cp in hid_copies(0):
        cp.start()

    def load_w1(n, _):
        for cp in w1_copies(n):
            cp.start()
        return 0
    lax.fori_loop(0, ft, load_w1, 0)
    w2_copy().start()

    barrier = pltpu.get_barrier_semaphore()

    def greet(d, _):
        peer = (me + d) % GROUP
        pl.semaphore_signal(barrier, inc=1, device_id=(dp, peer // 4, peer % 4), device_id_type=MESH)
        return 0
    lax.fori_loop(1, GROUP, greet, 0)

    def gate_up(at, width):
        both = jnp.dot(hid[...], w1[:, pl.ds(at, width)], preferred_element_type=F32)
        for b in range(width // 256):
            g = both[:, b * 256:b * 256 + 128]
            up = both[:, b * 256 + 128:b * 256 + 256]
            if isinstance(at, int):
                cols = pl.ds(at // 2 + b * 128, 128)
            else:
                cols = pl.ds(pl.multiple_of(at // 2 + b * 128, 128), 128)
            act[:, cols] = (jax.nn.silu(g) * up).astype(BF16)

    def down(i, at, width):
        cols = pl.ds(at, width)
        out = jnp.dot(act[...], w2[:, cols], preferred_element_type=F32).astype(BF16)
        acc[i, :, cols] = out[:HALF]
        dsend[:, cols] = out[HALF:]

    def mlp_step(i, j):
        per = -(-ft // 4)
        if j == 0:
            for cp in hid_copies(i):
                cp.wait()
        if j < 4:
            lo, hi = j * per, min(j * per + per, ft)
            if hi > lo:
                gate_up(lo * 256, (hi - lo) * 256)
        if j == 3:
            @pl.when(i + 1 < num_chunks)
            def _():
                for cp in hid_copies(i + 1):
                    cp.start()
        if j == 4:
            d_copy(i - 1, 0).wait_send()
            d_copy(i - 1, 1).wait_send()
        if j >= 4:
            for b in range(2):
                down(i, (j - 4) * (dim // 2) + b * (dim // 4), dim // 4)
            d_copy(i, j - 4).start()

    for cp in hid_copies(0):
        cp.wait()

    def first_tile(n, _):
        for cp in w1_copies(n):
            cp.wait()
        gate_up(pl.multiple_of(n * 256, 256), 256)
        return 0
    lax.fori_loop(0, ft, first_tile, 0)
    for cp in hid_copies(1):
        cp.start()
    w2_copy().wait()
    wv_copy(0).start()
    wv_copy(1).start()
    pl.semaphore_wait(barrier, GROUP - 1)

    def first_down(part, _):
        for b in range(2):
            at = pl.multiple_of(part * (dim // 2) + b * (dim // 4), dim // 4)
            down(0, at, dim // 4)
        d_copy(0, part).start()
        return 0
    lax.fori_loop(0, 2, first_down, 0)

    def column(row_ref, i, h):
        r = row_ref[pl.ds(2 * i + (c if h == 0 else 1 - c), 1), :].astype(F32)
        return jnp.transpose(jnp.broadcast_to(r, (128, 128)))

    lanes = 128
    rb = 32

    def vocab_step(i, q):
        n = i * 4 + q
        lslot = logits.at[i % 2]
        if q == 0:
            for k in range(UNITS):
                xd_copy((i, k), KINDS[k]).wait_recv()
        wv_copy(n).wait()
        col = q * vt
        lslot[:, pl.ds(col, vt)] = jnp.dot(xbuf[i], wv[q % 2], preferred_element_type=F32)

        @pl.when(n + 2 < num_chunks * 4)
        def _():
            wv_copy(n + 2).start()

        if q == 0:
            for h in range(2):
                r = pl.ds(h * HALF, HALF)
                stat[0, r] = jnp.full((HALF, lanes), -jnp.inf, F32)
                stat[1, r] = jnp.zeros((HALF, lanes), F32)
                stat[2, r] = jnp.zeros((HALF, lanes), F32)
                stat[3, r] = jnp.zeros((HALF, lanes), F32)
                stat[4, r] = 1.0 / column(temp, i, h)
                stat[5, r] = column(ids, i, h) - (me * vocab).astype(F32)

        def block(b, _):
            r = pl.ds(pl.multiple_of(b * rb, rb), rb)
            inv_t = stat[4, r]
            want = stat[5, r] - lax.broadcasted_iota(jnp.int32, (rb, lanes), 1).astype(F32) - float(q * vt)
            old = stat[0, r]
            top = old
            parts = []
            target = stat[3, r]
            for g in range(vt // lanes):
                cols = pl.ds(col + g * lanes, lanes)
                lg = lslot[r, cols] * inv_t
                lslot[r, cols] = lg
                top = jnp.maximum(top, lg)
                target = target + jnp.where(want == float(g * lanes), lg, 0.0)
                parts.append(lg)
            scale = jnp.exp(old - top)
            total = stat[1, r] * scale
            moment = stat[2, r] * scale
            for lg in parts:
                e = jnp.exp(lg - top)
                total = total + e
                moment = moment + e * lg
            stat[0, r] = top
            stat[1, r] = total
            stat[2, r] = moment
            stat[3, r] = target
            return 0
        lax.fori_loop(0, CHUNK // rb, block, 0)

        if q == 3:
            for h in range(2):
                r = pl.ds(h * HALF, HALF)
                top = stat[0, r]
                best = jnp.max(top, axis=-1, keepdims=True)
                w = jnp.exp(top - best)
                total = jnp.sum(stat[1, r] * w, axis=-1, keepdims=True)
                moment = jnp.sum(stat[2, r] * w, axis=-1, keepdims=True)
                target = jnp.sum(stat[3, r], axis=-1, keepdims=True)
                lane = lax.broadcasted_iota(jnp.int32, (HALF, lanes), 1)
                packed = jnp.where(lane == 0, best, jnp.where(lane == 1, total, jnp.where(lane == 2, moment, target)))
                turned = jnp.transpose(packed)[:4]
                at = pl.multiple_of((c if h == 0 else 1 - c) * 4, 4)
                sbuf[i, 0, pl.ds(at, 4), :] = turned
            for d in range(1, GROUP):
                s_copy(i, d).start()

    def final_step(i):
        s_wait(i).wait_recv()
        for h in range(2):
            def pick(d, n):
                return sbuf[i, d, 4 * h + n:4 * h + n + 1, :]
            top = pick(0, 0)
            for d in range(1, GROUP):
                top = jnp.maximum(top, pick(d, 0))
            total = jnp.zeros((1, HALF), F32)
            moment = jnp.zeros((1, HALF), F32)
            target = jnp.zeros((1, HALF), F32)
            for d in range(GROUP):
                w = jnp.exp(pick(d, 0) - top)
                total = total + w * pick(d, 1)
                moment = moment + w * pick(d, 2)
                target = target + pick(d, 3)
            norm = top + jnp.log(total)
            r = pl.ds(2 * i + h, 1)
            log_norm[r, :] = norm
            entropy[r, :] = norm - moment / total
            target_logp[r, :] = target - norm

        @pl.when(i > 0)
        def _():
            for cp in out_copies(i - 1):
                cp.wait()
        for h in range(2):
            row = column(log_norm, i, h)
            stat[6, pl.ds(h * HALF, HALF)] = row

        def block(b, _):
            r = pl.ds(pl.multiple_of(b * rb, rb), rb)
            ln = stat[6, r]
            for g in range(vocab // lanes):
                cols = pl.ds(g * lanes, lanes)
                outb[r, cols] = (logits[i % 2, r, cols] - ln).astype(BF16)
            return 0
        lax.fori_loop(0, CHUNK // rb, block, 0)
        for cp in out_copies(i):
            cp.start()

    def first(kind, u):
        i, k, rs, mr, zo = geo(u, kind)
        if kind == 'A':
            if k == 0:
                d_copy(i, 0).wait_recv()
                d_copy(i, 1).wait_recv()
            add_rows(i, rs, 2 * PIECE, drecv.at[i, rows(rs, 2 * PIECE)])
            ya_copy(u).start()
        else:
            add_rows(i, rs, PIECE, drecv.at[i, rows(rs)])

            @pl.when(dist(zo) == 3)
            def _():
                z_copy(u, kind).start()

    def after_ya(u):
        i, k, rs, mr, zo = geo(u, 'A')
        ya_copy(u).wait_recv()
        add_rows(i, mr, PIECE, ybuf.at[y_index(i, k, 'A')])

        @pl.when(dist(zo) == 3)
        def _():
            z_copy(u, 'A').start()

    def relay_sum(kind, u, at):
        i, k, rs, mr, zo = geo(u, kind)

        @pl.when(dist(zo) == at)
        def _():
            z_copy(u, kind).wait_recv()
            add_rows(i, mr, PIECE, zbuf.at[flat(u)])
            z_copy(u, kind).start()
        if at == 1:
            @pl.when(dist(zo) == 0)
            def _():
                hres_copy(u, kind).start()

    def owner_sum(u):
        kind = 'B'
        i, k, rs, mr, zo = geo(u, kind)

        @pl.when(dist(zo) == 0)
        def _():
            z_copy(u, 'B').wait_recv()
            add_rows(i, mr, PIECE, zbuf.at[flat(u)])
            yb_copy(u, kind).start()

    def owner_norm(kind, u):
        i, k, rs, mr, zo = geo(u, kind)

        @pl.when(dist(zo) == 0)
        def _():
            if kind == 'A':
                z_copy(u, kind).wait_recv()
                norm_rows(u, kind, zbuf.at[flat(u)])
                x_copy(u, kind).start()
                xy_copy(u).start()
            else:
                yb_copy(u, kind).wait_recv()
                norm_rows(u, kind, ybuf.at[y_index(i, k, 'B')])
                x_copy(u, kind).start()
                xd_copy(u, kind).start()

    def relay_x(kind, u, at):
        i, k, rs, mr, zo = geo(u, kind)

        @pl.when(dist(zo) == at)
        def _():
            x_copy(u, kind).wait_recv()
            if at < 3:
                x_copy(u, kind).start()
            if kind == 'A':
                xy_copy(u).start()
            else:
                xd_copy(u, kind).start()

    def after_xy(u):
        xy_wait(u).wait_recv()
        xd_copy(u, 'A').start()

    def first_c(u):
        i, k, rs, mr, zo = geo(u, 'C')
        add_rows(i, rs, PIECE, drecv.at[i, rows(rs)])

        @pl.when(z == 3 * (2 - zo))
        def _():
            z_copy(u, 'C').start()

        @pl.when(z == 3 * (zo - 1))
        def _():
            c_copy(u).start()

    def relay_c(u):
        i, k, rs, mr, zo = geo(u, 'C')

        @pl.when(z == 3 - zo)
        def _():
            z_copy(u, 'C').wait_recv()
            add_rows(i, mr, PIECE, zbuf.at[flat(u)])
            z_copy(u, 'C').start()

        @pl.when(z == zo)
        def _():
            hres_copy(u, 'C').start()

    def owner_sum_c(u):
        kind = 'C'
        i, k, rs, mr, zo = geo(u, kind)

        @pl.when(z == zo)
        def _():
            z_copy(u, kind).wait_recv()
            c_copy(u).wait_recv()
            add_rows(i, mr, PIECE, zbuf.at[flat(u)], cbuf.at[i])
            yb_copy(u, kind).start()

    def owner_norm_c(u):
        kind = 'C'
        i, k, rs, mr, zo = geo(u, kind)

        @pl.when(z == zo)
        def _():
            yb_copy(u, kind).wait_recv()
            norm_rows(u, kind, ybuf.at[y_index(i, k, kind)])
            x_copy(u, kind).start()
            xn_copy(u).start()
            xd_copy(u, kind).start()

    def relay_x_c(u):
        i, k, rs, mr, zo = geo(u, 'C')

        @pl.when(z == 3 - zo)
        def _():
            x_copy(u, 'C').wait_recv()
            x_copy(u, 'C').start()
            xd_copy(u, 'C').start()

        @pl.when(z == 3 * (zo - 1))
        def _():
            x_copy(u, 'C').wait_recv()
            xd_copy(u, 'C').start()

    def far_x_c(u):
        i, k, rs, mr, zo = geo(u, 'C')

        @pl.when(z == 3 * (2 - zo))
        def _():
            x_copy(u, 'C').wait_recv()
            xd_copy(u, 'C').start()

    def part(f, *fixed, **named):
        return functools.partial(f, *fixed, **named)

    steps_a = (part(first, 'A'), after_ya, part(relay_sum, 'A', at=2), part(relay_sum, 'A', at=1),
               part(owner_norm, 'A'), part(relay_x, 'A', at=1), part(relay_x, 'A', at=2), part(relay_x, 'A', at=3),
               after_xy)
    steps_b = (part(first, 'B'), part(relay_sum, 'B', at=2), part(relay_sum, 'B', at=1), owner_sum,
               part(owner_norm, 'B'), part(relay_x, 'B', at=1), part(relay_x, 'B', at=2), part(relay_x, 'B', at=3))
    steps_c = (first_c, relay_c, owner_sum_c, owner_norm_c, relay_x_c, far_x_c)

    steps = {'A': steps_a, 'B': steps_b, 'C': steps_c}
    table = []
    for k in range(UNITS):
        for h, at in enumerate(POS_UNIT[k]):
            table.append((at % UNITS, at // UNITS, 0, steps[KINDS[k]][h], k))
    for j, at in enumerate(POS_MLP):
        table.append((at % UNITS, at // UNITS, 1, mlp_step, j))
    for q, at in enumerate(POS_VOCAB):
        table.append((at % UNITS, at // UNITS, 0, vocab_step, q))
    table.append((POS_FINAL % UNITS, POS_FINAL // UNITS, 0, final_step, None))
    table.sort(key=lambda row: row[:2])

    def one(i, body, n):
        if n is None:
            body(i)
        elif body in (mlp_step, vocab_step):
            body(i, n)
        else:
            body((i, n))

    def one_pass(it, _):
        for _, late, low, body, n in table:
            i = it - int(late)

            @pl.when((i >= low) & (i < num_chunks))
            def _():
                one(i, body, n)
        return 0

    passes = num_chunks + max(int(row[1]) for row in table)
    lax.fori_loop(0, passes, one_pass, 0)

    for cp in out_copies(num_chunks - 1):
        cp.wait()
    d_copy(num_chunks - 1, 0).wait_send()
    d_copy(num_chunks - 1, 1).wait_send()

    def drain_unit(u, kind):
        i, k, rs, mr, zo = geo(u, kind)
        xd_copy(u, kind).wait_send()
        if kind == 'A':
            ya_copy(u).wait_send()
            xy_copy(u).wait_send()
        own = dist(zo) == 0
        if kind == 'C':
            own = z == zo

        @pl.when(jnp.logical_not(own))
        def _():
            z_copy(u, kind).wait_send()

        @pl.when((own | (z == 3 - zo)) if kind == 'C' else dist(zo) < 3)
        def _():
            x_copy(u, kind).wait_send()

        if kind != 'A':
            @pl.when(own)
            def _():
                yb_copy(u, kind).wait_send()
                if kind == 'C':
                    xn_copy(u).wait_send()

    def drain(n, _):
        for k in range(UNITS):
            drain_unit((n, k), KINDS[k])
        return 0
    lax.fori_loop(0, num_chunks, drain, 0)

    def drain_stats(i, _):
        s_wait(i).wait_send()
        return 0
    lax.fori_loop(0, num_chunks, drain_stats, 0)


def finish(logprobs, log_norm, entropy, target_logp, out, a, b, d, block, load_sem, store_sem):
    a[...] = log_norm[...]
    b[...] = entropy[...]
    d[...] = target_logp[...]
    n, size = block.shape[0], block.shape[1]
    loads = [pltpu.make_async_copy(logprobs.at[pl.ds(j * size, size)], block.at[j], load_sem.at[j]) for j in range(n)]
    stores = [pltpu.make_async_copy(block.at[j], out.at[pl.ds(j * size, size)], store_sem.at[j]) for j in range(n)]
    for cp in loads:
        cp.start()
    for j in range(n):
        loads[j].wait()
        stores[j].start()
    for cp in stores:
        cp.wait()


def hand_over(logprobs, log_norm, entropy, target_logp):
    rows, vocab = logprobs.shape
    n = 8
    vm = pl.BlockSpec(memory_space=pltpu.VMEM)
    hbm = pl.BlockSpec(memory_space=pl.ANY)
    small = jax.ShapeDtypeStruct(log_norm.shape, F32)
    return pl.pallas_call(
        finish,
        out_shape=(jax.ShapeDtypeStruct((rows, vocab), BF16), small, small, small),
        in_specs=[hbm, vm, vm, vm],
        out_specs=(hbm, vm, vm, vm),
        scratch_shapes=[pltpu.VMEM((n, rows // n, vocab), BF16), pltpu.SemaphoreType.DMA((n,)),
                        pltpu.SemaphoreType.DMA((n,))],
        name='hand_over',
    )(logprobs, log_norm, entropy, target_logp)


def fused(hidden, w_gate, w_up, w_down, gain, w_vocab, temp, ids):
    rows, dim = hidden.shape
    ff = w_gate.shape[1]
    vocab = w_vocab.shape[1]
    nc = rows // CHUNK
    nu = nc * UNITS
    vm = pl.BlockSpec(memory_space=pltpu.VMEM)
    hbm = pl.BlockSpec(memory_space=pl.ANY)
    dma = pltpu.SemaphoreType.DMA
    small = jax.ShapeDtypeStruct((rows // 128, 128), F32)
    return pl.pallas_call(
        functools.partial(kernel, nc),
        out_shape=(jax.ShapeDtypeStruct((rows, vocab), BF16), small, small, small),
        in_specs=[hbm, hbm, hbm, hbm, vm, hbm, vm, vm],
        out_specs=(hbm, vm, vm, vm),
        scratch_shapes=[
            pltpu.VMEM((dim, 2 * ff), BF16),
            pltpu.VMEM((ff, dim), BF16),
            pltpu.VMEM((2, dim, vocab // 4), BF16),
            pltpu.VMEM((CHUNK, dim), BF16),
            pltpu.VMEM((CHUNK, ff), BF16),
            pltpu.VMEM((HALF, dim), BF16),
            pltpu.VMEM((nc, HALF, dim), BF16),
            pltpu.VMEM((nc, HALF, dim), BF16),
            pltpu.VMEM((nu, PIECE, dim), BF16),
            pltpu.VMEM((nc, PIECE, dim), BF16),
            pltpu.VMEM((nc * 4, PIECE, dim), BF16),
            pltpu.VMEM((nc, CHUNK, dim), BF16),
            pltpu.VMEM((12, PIECE, dim), BF16),
            pltpu.VMEM((2, CHUNK, vocab), F32),
            pltpu.VMEM((7, CHUNK, 128), F32),
            pltpu.VMEM((nc, GROUP, 8, HALF), F32),
            pltpu.VMEM((CHUNK, vocab), BF16),
            dma((ff // 128, 2)), dma, dma((2,)), dma((2,)), dma((12,)), dma((2,)), dma((2,)), dma((nc, 2)),
            dma((nu,)), dma((nc * 4,)), dma((nu,)), dma((nu,)), dma((nc,)), dma((nu, 2)), dma((nu,)),
            dma((nu // 3,)), dma((nu,)), dma((nu,)), dma((nc,)), dma((nc,)),
        ],
        compiler_params=pltpu.CompilerParams(collective_id=0, has_side_effects=True, vmem_limit_bytes=67043328),
        cost_estimate=pl.CostEstimate(flops=2 * rows * dim * (3 * ff + vocab),
                                      bytes_accessed=2 * dim * (3 * ff + 4 * vocab + rows),
                                      transcendentals=rows * vocab),
        name='step_tail',
    )(hidden, w_gate, w_up, w_down, gain, w_vocab, temp, ids)


def solution(mesh):
    model_axes = ('tp2', 'tp')

    def local_step(hidden, w_gate, w_up, w_down, norm_gain, w_vocab, temperature, target_ids):
        rows = hidden.shape[0]
        logprobs, log_norm, entropy, target_logp = fused(
            hidden, w_gate, w_up, w_down, norm_gain[None, :], w_vocab,
            temperature.reshape(rows // 128, 128), target_ids.reshape(rows // 128, 128))
        logprobs, log_norm, entropy, target_logp = hand_over(logprobs, log_norm, entropy, target_logp)
        return log_norm.reshape(rows), entropy.reshape(rows), target_logp.reshape(rows), logprobs

    return jax.shard_map(
        local_step, mesh=mesh,
        in_specs=(P('dp', None), P(None, model_axes), P(None, model_axes), P(model_axes, None),
                  P(None), P(None, model_axes), P('dp'), P('dp')),
        out_specs=(P('dp'), P('dp'), P('dp'), P('dp', model_axes)),
        check_vma=False)
```

time: 167 us -> 134 us (0.80)
  Pallas kernels: 158 us -> 133 us
  local copies, waits for them, and re-layouts: 8.59 us -> 0 us
    pallas_call x1, Pallas kernels: 158 us -> 129 us  [fused(): pl.pallas_call(functools.partial(kernel, nc), out_shape=(jax.ShapeDtypeSt...]
    unnamed x4 -> x0, local copies, waits for them, and re-layouts: 8.59 us -> none
    pallas_call x0 -> x1, Pallas kernels: none -> 4.88 us  [hand_over(): pl.pallas_call(finish, out_shape=(jax.ShapeDtypeStruct((rows, vocab), BF1...]
where the time goes in v2:
time: 134 us
  Pallas kernels  133 us (99%)
    pallas_call x1, Pallas kernels, fused(): pl.pallas_call(functools.partial(kernel, nc), out_shape=(jax.ShapeDtypeSt...  129 us
    pallas_call x1, Pallas kernels, hand_over(): pl.pallas_call(finish, out_shape=(jax.ShapeDtypeStruct((rows, vocab), BF1...  4.88 us

profile of v2, /device:TPU:0, one launch (start us, length us, event | category | flops | bytes accessed | tf_op | source)
XLA Modules:
  0.0 134.1 jit_solution(8915367197551145828)
XLA Ops:
  0.6 128.6 %step_tail.1 = (bf16[1024,2048]{1,0:T(8,128)(2,1)}, f32[8,128]{1,0:T(8,128)}, f32[8,128]{1,0:T(8,128)}, f32[8,128]{1,0:T(8,128)}) custom-call(bf16[1024,4096]{1,0:T(8,128)(2,1)} %hidden.1, bf16[4096,896]{1,0:T(8,128)(2,1)} %w_gate.1, bf16[4096,896]{1,0:T(8,128)(2,1)} %w_up.1, bf16[896,4096]{1,0:T(8,128)(2,1)} %w_down.1, f32[1,4096]{1,0:T(1,128)} %bitcast.6, ...), custom_call_target="tpu_custom_call" | custom-call | flops 39728447488 | bytes 97517568 | tf_op jit(solution)/shard_map/step_tail/pallas_call | solution.py:676
  129.2 4.9 %hand_over.1 = (bf16[1024,2048]{1,0:T(8,128)(2,1)}, f32[8,128]{1,0:T(8,128)}, f32[8,128]{1,0:T(8,128)}, f32[8,128]{1,0:T(8,128)}) custom-call(bf16[1024,2048]{1,0:T(8,128)(2,1)} %get-tuple-element.12.logprobs, f32[8,128]{1,0:T(8,128)} %get-tuple-element.13.log_norm, f32[8,128]{1,0:T(8,128)} %get-tuple-element.14.entropy, f32[8,128]{1,0:T(8,128)} %get-tuple-element.15.target_logp), custom_call_target="tpu_custom_call" | custom-call | tf_op jit(solution)/shard_map/hand_over/pallas_call | solution.py:655

commit v3 on v2

--- a/solution.py
+++ b/solution.py
@@ -28,7 +28,7 @@
 )
 POS_MLP = (0.197, 1.967, 2.361, 2.656, 4.328, 4.82)
 POS_VOCAB = (48, 49.082, 50.459, 53.41)
-POS_FINAL = 57.836
+POS_FINAL = 59.7
 
 def kernel(num_chunks, hidden, w_gate, w_up, w_down, gain, w_vocab, temp, ids,
            logprobs, log_norm, entropy, target_logp,
@@ -64,8 +64,9 @@
         return (pltpu.make_async_copy(w_gate.at[:, pl.ds(col, 128)], w1.at[:, pl.ds(at, 128)], w_sem.at[n, 0]),
                 pltpu.make_async_copy(w_up.at[:, pl.ds(col, 128)], w1.at[:, pl.ds(at + 128, 128)], w_sem.at[n, 1]))
 
-    def w2_copy():
-        return pltpu.make_async_copy(w_down, w2, w2_sem)
+    def w2_copy(n):
+        cols = pl.ds(pl.multiple_of(n * (dim // 4), dim // 4), dim // 4)
+        return pltpu.make_async_copy(w_down.at[:, cols], w2.at[:, cols], w2_sem.at[n])
 
     def wv_copy(n):
         q = n % 4
@@ -88,10 +89,18 @@
         return pltpu.make_async_remote_copy(src_ref=src, dst_ref=dst, send_sem=send, recv_sem=recv,
                                             device_id=dev, device_id_type=MESH)
 
-    def d_copy(i, part):
-        start = part * (dim // 2)
-        cols = pl.ds(start if isinstance(part, int) else pl.multiple_of(start, dim // 2), dim // 2)
+    def d_copy(i, part, pieces):
+        width = dim // pieces
+        start = part * width
+        cols = pl.ds(start if isinstance(part, int) else pl.multiple_of(start, width), width)
         return remote(dsend.at[:, cols], drecv.at[i, :, cols], d_send.at[part], d_recv.at[i, part], core_dev)
+
+    def d_wait(i, what):
+        for pieces in (4, 2):
+            @pl.when((i == 0) if pieces == 4 else (i > 0))
+            def _():
+                for b in range(pieces):
+                    getattr(d_copy(i, b, pieces), what)()
 
     def geo(u, kind):
         i, k = u
@@ -205,7 +214,6 @@
             cp.start()
         return 0
     lax.fori_loop(0, ft, load_w1, 0)
-    w2_copy().start()
 
     barrier = pltpu.get_barrier_semaphore()
 
@@ -247,12 +255,11 @@
                 for cp in hid_copies(i + 1):
                     cp.start()
         if j == 4:
-            d_copy(i - 1, 0).wait_send()
-            d_copy(i - 1, 1).wait_send()
+            d_wait(i - 1, 'wait_send')
         if j >= 4:
-            for b in range(2):
-                down(i, (j - 4) * (dim // 2) + b * (dim // 4), dim // 4)
-            d_copy(i, j - 4).start()
+            for b in range(2 * (j - 4), 2 * (j - 4) + 2):
+                down(i, b * (dim // 4), dim // 4)
+            d_copy(i, j - 4, 2).start()
 
     for cp in hid_copies(0):
         cp.wait()
@@ -260,23 +267,24 @@
     def first_tile(n, _):
         for cp in w1_copies(n):
             cp.wait()
+        @pl.when(n >= ft - 4)
+        def _():
+            w2_copy(n - (ft - 4)).start()
         gate_up(pl.multiple_of(n * 256, 256), 256)
         return 0
     lax.fori_loop(0, ft, first_tile, 0)
     for cp in hid_copies(1):
         cp.start()
-    w2_copy().wait()
+    pl.semaphore_wait(barrier, GROUP - 1)
+
+    def first_down(part, _):
+        w2_copy(part).wait()
+        down(0, pl.multiple_of(part * (dim // 4), dim // 4), dim // 4)
+        d_copy(0, part, 4).start()
+        return 0
+    lax.fori_loop(0, 4, first_down, 0)
     wv_copy(0).start()
     wv_copy(1).start()
-    pl.semaphore_wait(barrier, GROUP - 1)
-
-    def first_down(part, _):
-        for b in range(2):
-            at = pl.multiple_of(part * (dim // 2) + b * (dim // 4), dim // 4)
-            down(0, at, dim // 4)
-        d_copy(0, part).start()
-        return 0
-    lax.fori_loop(0, 2, first_down, 0)
 
     def column(row_ref, i, h):
         r = row_ref[pl.ds(2 * i + (c if h == 0 else 1 - c), 1), :].astype(F32)
@@ -400,8 +408,7 @@
         i, k, rs, mr, zo = geo(u, kind)
         if kind == 'A':
             if k == 0:
-                d_copy(i, 0).wait_recv()
-                d_copy(i, 1).wait_recv()
+                d_wait(i, 'wait_recv')
             add_rows(i, rs, 2 * PIECE, drecv.at[i, rows(rs, 2 * PIECE)])
             ya_copy(u).start()
         else:
@@ -590,8 +597,7 @@
 
     for cp in out_copies(num_chunks - 1):
         cp.wait()
-    d_copy(num_chunks - 1, 0).wait_send()
-    d_copy(num_chunks - 1, 1).wait_send()
+    d_wait(num_chunks - 1, 'wait_send')
 
     def drain_unit(u, kind):
         i, k, rs, mr, zo = geo(u, kind)
@@ -696,7 +702,7 @@
             pltpu.VMEM((7, CHUNK, 128), F32),
             pltpu.VMEM((nc, GROUP, 8, HALF), F32),
             pltpu.VMEM((CHUNK, vocab), BF16),
-            dma((ff // 128, 2)), dma, dma((2,)), dma((2,)), dma((12,)), dma((2,)), dma((2,)), dma((nc, 2)),
+            dma((ff // 128, 2)), dma((4,)), dma((2,)), dma((2,)), dma((12,)), dma((2,)), dma((4,)), dma((nc, 4)),
             dma((nu,)), dma((nc * 4,)), dma((nu,)), dma((nu,)), dma((nc,)), dma((nu, 2)), dma((nu,)),
             dma((nu // 3,)), dma((nu,)), dma((nu,)), dma((nc,)), dma((nc,)),
         ],

time: 134 us -> 134 us (level)
  no operation moved by 1% of the time
where the time goes in v3:
time: 134 us; the launch traced here: 133 us
  Pallas kernels  133 us (99%)
    pallas_call x1, Pallas kernels, fused(): pl.pallas_call(functools.partial(kernel, nc), out_shape=(jax.ShapeDtypeSt...  128 us
    pallas_call x1, Pallas kernels, hand_over(): pl.pallas_call(finish, out_shape=(jax.ShapeDtypeStruct((rows, vocab), BF1...  4.88 us

profile of v3, /device:TPU:0, one launch (start us, length us, event | category | flops | bytes accessed | tf_op | source)
XLA Modules:
  0.0 133.3 jit_solution(9048035211052329303)
XLA Ops:
  0.6 127.8 %step_tail.1 = (bf16[1024,2048]{1,0:T(8,128)(2,1)}, f32[8,128]{1,0:T(8,128)}, f32[8,128]{1,0:T(8,128)}, f32[8,128]{1,0:T(8,128)}) custom-call(bf16[1024,4096]{1,0:T(8,128)(2,1)} %hidden.1, bf16[4096,896]{1,0:T(8,128)(2,1)} %w_gate.1, bf16[4096,896]{1,0:T(8,128)(2,1)} %w_up.1, bf16[896,4096]{1,0:T(8,128)(2,1)} %w_down.1, f32[1,4096]{1,0:T(1,128)} %bitcast.6, ...), custom_call_target="tpu_custom_call" | custom-call | flops 39728447488 | bytes 97517568 | tf_op jit(solution)/shard_map/step_tail/pallas_call | solution.py:682
  128.4 4.9 %hand_over.1 = (bf16[1024,2048]{1,0:T(8,128)(2,1)}, f32[8,128]{1,0:T(8,128)}, f32[8,128]{1,0:T(8,128)}, f32[8,128]{1,0:T(8,128)}) custom-call(bf16[1024,2048]{1,0:T(8,128)(2,1)} %get-tuple-element.12.logprobs, f32[8,128]{1,0:T(8,128)} %get-tuple-element.13.log_norm, f32[8,128]{1,0:T(8,128)} %get-tuple-element.14.entropy, f32[8,128]{1,0:T(8,128)} %get-tuple-element.15.target_logp), custom_call_target="tpu_custom_call" | custom-call | tf_op jit(solution)/shard_map/hand_over/pallas_call | solution.py:661
